TPU v7x, 32 devices: a whole 2x2x4 slice. The times are simulated.
32 devices in a mesh: dp: 8 (over y, x, core), tensor: 4 (over z).
Axes of the slice: x: 2, y: 2, z: 4, core: 2. Of those that a mesh axis runs over, the one named last changes fastest.
Arguments:
- tokens: bfloat16 [8192, 1280], P(('dp', 'tensor')), may hold values from -6 to 6
- w_query: bfloat16 [1280, 1280], P('dp', 'tensor'), may hold values from -0.15625 to 0.15625
- w_key: bfloat16 [1280, 1280], P('dp', 'tensor'), may hold values from -0.15625 to 0.15625
- w_value: bfloat16 [1280, 1280], P('dp', 'tensor'), may hold values from -0.15625 to 0.15625
- w_out: bfloat16 [1280, 1280], P('dp', 'tensor'), may hold values from -0.15625 to 0.15625
- w_up: bfloat16 [1280, 5120], P('dp', 'tensor'), may hold values from -0.15625 to 0.15625
- w_gate: bfloat16 [1280, 5120], P('dp', 'tensor'), may hold values from -0.15625 to 0.15625
- w_down: bfloat16 [1280, 5120], P('dp', 'tensor'), may hold values from -0.078125 to 0.078125
- qk_scale: float32 [1280], P('tensor'), may hold values from 0.8 to 1.8
- up_scale: float32 [5120], P('tensor'), may hold values from 0.5 to 2
- gate_scale: float32 [5120], P('tensor'), may hold values from 0.5 to 2
- alpha_attn: float32 [1280], replicated, may hold values from 0.2 to 0.6
- alpha_mlp: float32 [1280], replicated, may hold values from 0.2 to 0.6
- cotangent: bfloat16 [8192, 1280], P(('dp', 'tensor')), may hold values from -6 to 6
Outputs:
- output: bfloat16 [8192, 1280], P(('dp', 'tensor'))
- tokens_gradient: float32 [8192, 1280], P(('dp', 'tensor'))
- w_query_gradient: float32 [1280, 1280], P('dp', 'tensor')
- w_key_gradient: float32 [1280, 1280], P('dp', 'tensor')
- w_value_gradient: float32 [1280, 1280], P('dp', 'tensor')
- w_out_gradient: float32 [1280, 1280], P('dp', 'tensor')
- w_up_gradient: float32 [1280, 5120], P('dp', 'tensor')
- w_gate_gradient: float32 [1280, 5120], P('dp', 'tensor')
- w_down_gradient: float32 [1280, 5120], P('dp', 'tensor')
- qk_scale_gradient: float32 [1280], P('tensor')
- up_scale_gradient: float32 [5120], P('tensor')
- gate_scale_gradient: float32 [5120], P('tensor')
- alpha_attn_gradient: float32 [1280], replicated
- alpha_mlp_gradient: float32 [1280], replicated
All inputs are finite; a program needn't handle non-finite values.
Results may differ from a plain program's by a relative error of at most 0.017.
Values may be sent and summed in bfloat16 or wider, within the bound.
A program may use at most 192 MiB of HBM per device.

v0:
```python
import jax
import jax.numpy as jnp
from jax import lax
from jax.sharding import PartitionSpec as P

HEAD_DIM = 64
HIGH = lax.Precision.HIGHEST
EPS = 1e-06


def unit_rows(value):
    scale = lax.rsqrt(jnp.mean(value * value, axis=-1, keepdims=True) + EPS)
    return (value * scale, scale)


def unit_back(grad, unit, scale):
    return scale * (grad - unit * jnp.mean(grad * unit, axis=-1, keepdims=True))


def contract_rows(left, right):
    return lax.dot_general(
        left, right, (((0,), (0,)), ((), ())), preferred_element_type=jnp.float32
    )


def contract_cols(left, right):
    return lax.dot_general(
        left, right, (((1,), (1,)), ((), ())), preferred_element_type=jnp.float32
    )


def tables(width, length):
    half_dim = HEAD_DIM // 2
    column = lax.iota(jnp.int32, width)
    within = column % HEAD_DIM
    freq_index = (within % half_dim).astype(jnp.float32)
    frequency = 10000.0 ** (-freq_index / half_dim)
    position = lax.iota(jnp.float32, length)
    angle = position[:, None] * frequency[None, :]
    first_half = (within < half_dim)[None, :]
    heads = width // HEAD_DIM
    member = (
        lax.broadcasted_iota(jnp.int32, (width, heads), 0) // HEAD_DIM
        == lax.broadcasted_iota(jnp.int32, (width, heads), 1)
    ).astype(jnp.float32)
    return (jnp.cos(angle), jnp.sin(angle), first_half, member)


def rope_apply(value, cosine, sine, first_half):
    half_dim = HEAD_DIM // 2
    turned = jnp.where(
        first_half, -jnp.roll(value, -half_dim, axis=1), jnp.roll(value, half_dim, axis=1)
    )
    return value * cosine + turned * sine


def rope_back(grad, cosine, sine, first_half):
    half_dim = HEAD_DIM // 2
    weighted = grad * sine
    turned = jnp.where(
        first_half, jnp.roll(weighted, -half_dim, axis=1), -jnp.roll(weighted, half_dim, axis=1)
    )
    return grad * cosine + turned


def head_unit(value, member):
    mean_sq = (
        jnp.dot(value * value, member, precision=HIGH, preferred_element_type=jnp.float32)
        / HEAD_DIM
    )
    scale = jnp.dot(
        lax.rsqrt(mean_sq + EPS), member.T, precision=HIGH, preferred_element_type=jnp.float32
    )
    return (value * scale, scale)


def head_back(grad, unit, scale, member):
    inner = (
        jnp.dot(grad * unit, member, precision=HIGH, preferred_element_type=jnp.float32) / HEAD_DIM
    )
    spread = jnp.dot(inner, member.T, precision=HIGH, preferred_element_type=jnp.float32)
    return scale * (grad - unit * spread)


def block_scores(query3, key3, start, stop, block):
    scale = HEAD_DIM ** (-0.5)
    scores = (
        jnp.einsum(
            "qhd,khd->hqk", query3[start:stop], key3[:stop], preferred_element_type=jnp.float32
        )
        * scale
    )
    allowed = start + lax.broadcasted_iota(jnp.int32, (block, stop), 0) >= lax.broadcasted_iota(
        jnp.int32, (block, stop), 1
    )
    return jnp.where(allowed[None], scores, -jnp.inf)


def attend(query3, key3, value3, block):
    length = query3.shape[0]
    outputs = []
    totals = []
    for block_id in range(length // block):
        start = block_id * block
        stop = start + block
        scores = block_scores(query3, key3, start, stop, block)
        row_max = jnp.max(scores, axis=-1, keepdims=True)
        log_total = jnp.log(jnp.sum(jnp.exp(scores - row_max), axis=-1, keepdims=True)) + row_max
        weights = jnp.exp(scores - log_total).astype(jnp.bfloat16)
        outputs.append(
            jnp.einsum("hqk,khd->qhd", weights, value3[:stop], preferred_element_type=jnp.float32)
        )
        totals.append(log_total)
    return (jnp.concatenate(outputs, axis=0), totals)


def attend_back(query3, key3, value3, grad3, totals, block):
    length = query3.shape[0]
    scale = HEAD_DIM ** (-0.5)
    query_parts = []
    key_grad = jnp.zeros(key3.shape, jnp.float32)
    value_grad = jnp.zeros(value3.shape, jnp.float32)
    for block_id in range(length // block):
        start = block_id * block
        stop = start + block
        scores = block_scores(query3, key3, start, stop, block)
        probs = jnp.exp(scores - totals[block_id])
        g_probs = jnp.einsum(
            "qhd,khd->hqk", grad3[start:stop], value3[:stop], preferred_element_type=jnp.float32
        )
        inner = jnp.sum(probs * g_probs, axis=-1, keepdims=True)
        g_scores = (probs * (g_probs - inner)).astype(jnp.bfloat16)
        query_parts.append(
            jnp.einsum("hqk,khd->qhd", g_scores, key3[:stop], preferred_element_type=jnp.float32)
            * scale
        )
        key_grad = key_grad.at[:stop].add(
            jnp.einsum(
                "hqk,qhd->khd", g_scores, query3[start:stop], preferred_element_type=jnp.float32
            )
            * scale
        )
        value_grad = value_grad.at[:stop].add(
            jnp.einsum(
                "hqk,qhd->khd",
                probs.astype(jnp.bfloat16),
                grad3[start:stop],
                preferred_element_type=jnp.float32,
            )
        )
    return (jnp.concatenate(query_parts, axis=0), key_grad, value_grad)


def gather_attention(w_query, w_key, w_value, w_out):
    return (
        lax.all_gather(w_query, "dp", axis=0, tiled=True),
        lax.all_gather(w_key, "dp", axis=0, tiled=True),
        lax.all_gather(w_value, "dp", axis=0, tiled=True),
        lax.all_gather(w_out, "dp", axis=0, tiled=True),
    )


def gather_feedforward(w_up, w_gate, w_down):
    return (
        lax.all_gather(w_up, "dp", axis=0, tiled=True),
        lax.all_gather(w_gate, "dp", axis=0, tiled=True),
        lax.all_gather(w_down, "dp", axis=0, tiled=True),
    )


def on_device(
    tokens,
    w_query,
    w_key,
    w_value,
    w_out,
    w_up,
    w_gate,
    w_down,
    qk_scale,
    up_scale,
    gate_scale,
    alpha_attn,
    alpha_mlp,
    cotangent,
):
    query_w, key_w, value_w, out_w = gather_attention(w_query, w_key, w_value, w_out)
    whole = lax.all_gather(tokens, "tensor", axis=0, tiled=True)
    length = whole.shape[0]
    width = query_w.shape[1]
    block = min(512, length)
    cosine, sine, first_half, member = tables(width, length)
    shape3 = (length, width // HEAD_DIM, HEAD_DIM)
    q_raw = jnp.dot(whole, query_w, preferred_element_type=jnp.float32)
    k_raw = jnp.dot(whole, key_w, preferred_element_type=jnp.float32)
    value_low = jnp.dot(whole, value_w, preferred_element_type=jnp.float32).astype(jnp.bfloat16)
    q_unit, q_norm = head_unit(rope_apply(q_raw, cosine, sine, first_half), member)
    k_unit, k_norm = head_unit(rope_apply(k_raw, cosine, sine, first_half), member)
    query_low = (q_unit * qk_scale).astype(jnp.bfloat16)
    key_low = (k_unit * qk_scale).astype(jnp.bfloat16)
    query3 = query_low.reshape(shape3)
    key3 = key_low.reshape(shape3)
    value3 = value_low.reshape(shape3)
    attended, totals = attend(query3, key3, value3, block)
    attended_low = attended.reshape(length, width).astype(jnp.bfloat16)
    attn_sum = lax.psum_scatter(
        contract_cols(attended_low, out_w), "tensor", scatter_dimension=0, tiled=True
    )
    attn_unit, attn_norm = unit_rows(attn_sum)
    residual = tokens.astype(jnp.float32)
    mid, mid_norm = unit_rows(residual + alpha_attn * (attn_unit - residual))
    mid_low = mid.astype(jnp.bfloat16)
    up_w, gate_w, down_w = gather_feedforward(w_up, w_gate, w_down)
    mid_whole = lax.all_gather(mid_low, "tensor", axis=0, tiled=True)
    up_sum = jnp.dot(mid_whole, up_w, preferred_element_type=jnp.float32)
    gate_sum = jnp.dot(mid_whole, gate_w, preferred_element_type=jnp.float32)
    up_val = up_sum * up_scale
    gate_val = gate_sum * gate_scale
    sigma = jax.nn.sigmoid(gate_val)
    hidden_low = (up_val * (gate_val * sigma)).astype(jnp.bfloat16)
    mlp_sum = lax.psum_scatter(
        contract_cols(hidden_low, down_w), "tensor", scatter_dimension=0, tiled=True
    )
    mlp_unit, mlp_norm = unit_rows(mlp_sum)
    final, final_norm = unit_rows(mid + alpha_mlp * (mlp_unit - mid))
    output = final.astype(jnp.bfloat16)
    g_second = unit_back(cotangent.astype(jnp.float32), final, final_norm)
    g_alpha_mlp = jnp.sum((mlp_unit - mid) * g_second, axis=0)
    g_mlp_low = unit_back(alpha_mlp * g_second, mlp_unit, mlp_norm).astype(jnp.bfloat16)
    up_w, gate_w, down_w = gather_feedforward(w_up, w_gate, w_down)
    g_mlp_whole = lax.all_gather(g_mlp_low, "tensor", axis=0, tiled=True)
    down_grad = contract_rows(g_mlp_whole, hidden_low)
    g_hidden = jnp.dot(g_mlp_whole, down_w, preferred_element_type=jnp.float32)
    g_up = g_hidden * (gate_val * sigma)
    g_gate = g_hidden * up_val * (sigma * (1.0 + gate_val * (1.0 - sigma)))
    up_scale_grad = jnp.sum(g_up * up_sum, axis=0)
    gate_scale_grad = jnp.sum(g_gate * gate_sum, axis=0)
    g_up_low = (g_up * up_scale).astype(jnp.bfloat16)
    g_gate_low = (g_gate * gate_scale).astype(jnp.bfloat16)
    up_grad = contract_rows(mid_whole, g_up_low)
    gate_grad = contract_rows(mid_whole, g_gate_low)
    g_mid_part = contract_cols(g_up_low, up_w) + contract_cols(g_gate_low, gate_w)
    g_mid = (1.0 - alpha_mlp) * g_second + lax.psum_scatter(
        g_mid_part, "tensor", scatter_dimension=0, tiled=True
    )
    up_grad, gate_grad, down_grad = (
        lax.psum_scatter(up_grad, "dp", scatter_dimension=0, tiled=True),
        lax.psum_scatter(gate_grad, "dp", scatter_dimension=0, tiled=True),
        lax.psum_scatter(down_grad, "dp", scatter_dimension=0, tiled=True),
    )
    g_first = unit_back(g_mid, mid, mid_norm)
    g_alpha_attn = jnp.sum((attn_unit - residual) * g_first, axis=0)
    g_attn_low = unit_back(alpha_attn * g_first, attn_unit, attn_norm).astype(jnp.bfloat16)
    query_w, key_w, value_w, out_w = gather_attention(w_query, w_key, w_value, w_out)
    g_attn_whole = lax.all_gather(g_attn_low, "tensor", axis=0, tiled=True)
    out_grad = contract_rows(g_attn_whole, attended_low)
    g_attended_low = jnp.dot(g_attn_whole, out_w, preferred_element_type=jnp.float32).astype(
        jnp.bfloat16
    )
    g_query3, g_key3, g_value3 = attend_back(
        query3, key3, value3, g_attended_low.reshape(shape3), totals, block
    )
    g_query = g_query3.reshape(length, width)
    g_key = g_key3.reshape(length, width)
    qk_grad = jnp.sum(g_query * q_unit, axis=0) + jnp.sum(g_key * k_unit, axis=0)
    g_q_raw_low = rope_back(
        head_back(g_query * qk_scale, q_unit, q_norm, member), cosine, sine, first_half
    ).astype(jnp.bfloat16)
    g_k_raw_low = rope_back(
        head_back(g_key * qk_scale, k_unit, k_norm, member), cosine, sine, first_half
    ).astype(jnp.bfloat16)
    g_value_low = g_value3.reshape(length, width).astype(jnp.bfloat16)
    query_grad = contract_rows(whole, g_q_raw_low)
    key_grad = contract_rows(whole, g_k_raw_low)
    value_grad = contract_rows(whole, g_value_low)
    g_tok_part = (
        contract_cols(g_q_raw_low, query_w)
        + contract_cols(g_k_raw_low, key_w)
        + contract_cols(g_value_low, value_w)
    )
    tokens_grad = (1.0 - alpha_attn) * g_first + lax.psum_scatter(
        g_tok_part.astype(jnp.bfloat16), "tensor", scatter_dimension=0, tiled=True
    ).astype(jnp.float32)
    query_grad, key_grad, value_grad, out_grad = (
        lax.psum_scatter(query_grad, "dp", scatter_dimension=0, tiled=True),
        lax.psum_scatter(key_grad, "dp", scatter_dimension=0, tiled=True),
        lax.psum_scatter(value_grad, "dp", scatter_dimension=0, tiled=True),
        lax.psum_scatter(out_grad, "dp", scatter_dimension=0, tiled=True),
    )
    qk_grad, up_scale_grad, gate_scale_grad = lax.psum(
        (qk_grad, up_scale_grad, gate_scale_grad), "dp"
    )
    g_alpha_attn, g_alpha_mlp = lax.psum((g_alpha_attn, g_alpha_mlp), ("dp", "tensor"))
    return (
        output,
        tokens_grad,
        query_grad,
        key_grad,
        value_grad,
        out_grad,
        up_grad,
        gate_grad,
        down_grad,
        qk_grad,
        up_scale_grad,
        gate_scale_grad,
        g_alpha_attn,
        g_alpha_mlp,
    )


def solution(mesh):
    in_specs = (
        P(("dp", "tensor"), None),
        P("dp", "tensor"),
        P("dp", "tensor"),
        P("dp", "tensor"),
        P("dp", "tensor"),
        P("dp", "tensor"),
        P("dp", "tensor"),
        P("dp", "tensor"),
        P("tensor"),
        P("tensor"),
        P("tensor"),
        P(),
        P(),
        P(("dp", "tensor"), None),
    )
    out_specs = (
        P(("dp", "tensor"), None),
        P(("dp", "tensor"), None),
        P("dp", "tensor"),
        P("dp", "tensor"),
        P("dp", "tensor"),
        P("dp", "tensor"),
        P("dp", "tensor"),
        P("dp", "tensor"),
        P("dp", "tensor"),
        P("tensor"),
        P("tensor"),
        P("tensor"),
        P(),
        P(),
    )
    return jax.shard_map(
        on_device, mesh=mesh, in_specs=in_specs, out_specs=out_specs, check_vma=False
    )
```

profile of v0, /device:TPU:0, one launch (start us, length us, event | category | flops | bytes accessed | tf_op | source)
XLA Modules:
  0.0 1157.3 jit_solution(15452497443347139287)
XLA Ops:
  9.0 12.8 %all_gather.41 = bf16[1280,320]{1,0:T(8,128)(2,1)S(1)} all-gather(bf16[160,320]{1,0:T(8,128)(2,1)} %param.29), channel_id=1, replica_groups=mesh['dp'=8,'tensor'=4] {'dp'}, dimensions={0}, use_global_device_ids=true | all-gather | bytes 921600 | tf_op jit(solution)/shard_map/all_gather | solution.py:158
  21.8 11.6 %all_gather.43 = bf16[1280,320]{1,0:T(8,128)(2,1)} all-gather(bf16[160,320]{1,0:T(8,128)(2,1)S(1)} %copy-done.50), channel_id=1, replica_groups=mesh['dp'=8,'tensor'=4] {'dp'}, dimensions={0}, use_global_device_ids=true | all-gather | bytes 921600 | tf_op jit(solution)/shard_map/all_gather | solution.py:157
  33.3 11.4 all_gather.42
  44.7 11.5 all_gather.44
  56.6 11.3 all-gather.8.cloned.1.call-done
  67.9 3.0 fusion.124
  74.3 6.5 fusion.20
  89.5 3.1 exponential_reduce_fusion
  96.0 2.9 fusion.67
  101.9 3.9 fusion.125
  106.4 92.1 %reduce-scatter.18.cloned.1.call-done = f32[256,1280]{1,0:T(8,128)} async-done(((f32[1024,1280]{1,0:T(8,128)}), f32[256,1280]{1,0:T(8,128)}) %reduce-scatter.18.cloned.1.call-update) | async-done | bytes 1310736 | tf_op jit(solution)/shard_map/reduce_scatter | solution.py:206
  204.5 53.4 %all-gather.10.cloned.1.call-done = bf16[1024,1280]{1,0:T(8,128)(2,1)} async-done(((bf16[256,1280]{1,0:T(8,128)(2,1)}), bf16[1024,1280]{1,0:T(8,128)(2,1)}) %all-gather.10.cloned.1.call-update) | async-done | bytes 2621456 | tf_op jit(solution)/shard_map/all_gather | solution.py:214
  257.8 8.6 fusion.126
  266.4 24.5 %all-gather.12.cloned.1.call-done = bf16[1280,1280]{1,0:T(8,128)(2,1)} async-done(((bf16[160,1280]{1,0:T(8,128)(2,1)}), bf16[1280,1280]{1,0:T(8,128)(2,1)}) %all-gather.12.cloned.1.call-update) | async-done | bytes 3276816 | tf_op jit(solution)/shard_map/all_gather | solution.py:165
  290.8 11.3 multiply_convert_fusion.4
  302.1 23.2 %all-gather.16.cloned.1.call-done = bf16[1280,1280]{1,0:T(8,128)(2,1)} async-done(((bf16[160,1280]{1,0:T(8,128)(2,1)}), bf16[1280,1280]{1,0:T(8,128)(2,1)}) %all-gather.16.cloned.1.call-update) | async-done | bytes 3276816 | tf_op jit(solution)/shard_map/all_gather | solution.py:167
  325.4 8.7 fusion.127
  334.1 93.9 %reduce-scatter.20.cloned.1.call-done = f32[256,1280]{1,0:T(8,128)} async-done(((f32[1024,1280]{1,0:T(8,128)}), f32[256,1280]{1,0:T(8,128)}) %reduce-scatter.20.cloned.1.call-update) | async-done | bytes 1310736 | tf_op jit(solution)/shard_map/reduce_scatter | solution.py:221
  435.4 54.5 %all-gather.18.cloned.1.call-done = bf16[1024,1280]{1,0:T(8,128)(2,1)} async-done(((bf16[256,1280]{1,0:T(8,128)(2,1)}), bf16[1024,1280]{1,0:T(8,128)(2,1)}) %all-gather.18.cloned.1.call-update) | async-done | bytes 2621456 | tf_op jit(solution)/shard_map/all_gather | solution.py:231
  490.0 11.1 multiply_reduce_fusion.1
  501.1 3.6 fusion.128
  505.5 5.4 convolution_add_fusion
  511.0 92.5 %reduce-scatter.22.cloned.1.call-done = f32[256,1280]{1,0:T(8,128)} async-done(((f32[1024,1280]{1,0:T(8,128)}), f32[256,1280]{1,0:T(8,128)}) %reduce-scatter.22.cloned.1.call-update) | async-done | bytes 1310736 | tf_op jit(solution)/shard_map/reduce_scatter | solution.py:243
  610.8 54.8 %all-gather.20.cloned.1.call-done = bf16[1024,1280]{1,0:T(8,128)(2,1)} async-done(((bf16[256,1280]{1,0:T(8,128)(2,1)}), bf16[1024,1280]{1,0:T(8,128)(2,1)}) %all-gather.20.cloned.1.call-update) | async-done | bytes 2621456 | tf_op jit(solution)/shard_map/all_gather | solution.py:255
  669.1 4.5 multiply_reduce_fusion.3
  673.7 4.2 multiply_convert_fusion.1
  680.1 3.9 multiply_reduce_fusion
  683.9 3.3 multiply_convert_fusion
  695.2 7.2 fusion.35
  705.3 6.0 fusion.24
  714.6 3.0 fusion.12
  718.4 3.3 add_convert_fusion
  721.9 8.9 fusion.132
  731.0 9.7 fusion.68
  740.8 8.8 fusion.133
  750.7 4.0 convolution_bitcast_fusion.2
  758.6 3.9 convolution_bitcast_fusion.1
  762.5 2.8 copy.48
  766.4 3.9 convolution_bitcast_fusion
  774.2 4.6 fusion.131
  778.8 39.5 %all-reduce.2 = (f32[1280]{0:T(1024)}, f32[1280]{0:T(1024)}) all-reduce(f32[1280]{0:T(1024)S(1)} %get-tuple-element.110, f32[1280]{0:T(1024)S(1)} %get-tuple-element.108), channel_id=1, replica_groups=mesh['dp'=8,'tensor'=4] {'dp','tensor'}, use_global_device_ids=true, to_apply=%region_33.34 | all-reduce | flops 2560 | bytes 20480 | tf_op jit(solution)/shard_map/psum | solution.py:293
  820.3 25.1 %all-reduce.3 = (f32[320]{0:T(512)}, f32[1280]{0:T(1024)}, f32[1280]{0:T(1024)}) all-reduce(f32[320]{0:T(512)S(1)} %add.253, f32[1280]{0:T(1024)S(1)} %get-tuple-element.107, f32[1280]{0:T(1024)S(1)} %get-tuple-element.106), channel_id=1, replica_groups=mesh['dp'=8,'tensor'=4] {'dp'}, use_global_device_ids=true, to_apply=%region_27.28 | all-reduce | flops 2880 | bytes 23040 | tf_op jit(solution)/shard_map/psum | solution.py:290
  847.7 59.1 %reduce-scatter.30.cloned.1.call-done = f32[160,1280]{1,0:T(8,128)} async-done(((f32[1280,1280]{1,0:T(8,128)}), f32[160,1280]{1,0:T(8,128)}) %reduce-scatter.30.cloned.1.call-update) | async-done | bytes 819216 | tf_op jit(solution)/shard_map/reduce_scatter | solution.py:248
  906.8 66.9 %reduce-scatter.32.cloned.1.call-done = f32[160,1280]{1,0:T(8,128)} async-done(((f32[1280,1280]{1,0:T(8,128)}), f32[160,1280]{1,0:T(8,128)}) %reduce-scatter.32.cloned.1.call-update) | async-done | bytes 819216 | tf_op jit(solution)/shard_map/reduce_scatter | solution.py:249
  973.7 43.9 %reduce-scatter.34.cloned.1.call-done = f32[160,320]{1,0:T(8,128)} async-done(((f32[1280,320]{1,0:T(8,128)}), f32[160,320]{1,0:T(8,128)}) %reduce-scatter.34.cloned.1.call-update) | async-done | bytes 204816
  1017.6 44.1 %reduce-scatter.36.cloned.1.call-done = f32[160,320]{1,0:T(8,128)} async-done(((f32[1280,320]{1,0:T(8,128)}), f32[160,320]{1,0:T(8,128)}) %reduce-scatter.36.cloned.1.call-update) | async-done | bytes 204816
  1061.7 43.9 %reduce-scatter.38.cloned.1.call-done = f32[160,320]{1,0:T(8,128)} async-done(((f32[1280,320]{1,0:T(8,128)}), f32[160,320]{1,0:T(8,128)}) %reduce-scatter.38.cloned.1.call-update) | async-done | bytes 204816
  1105.6 44.1 %reduce-scatter.26.cloned.1.call-done = f32[160,320]{1,0:T(8,128)} async-done(((f32[1280,320]{1,0:T(8,128)}), f32[160,320]{1,0:T(8,128)}) %reduce-scatter.26.cloned.1.call-update) | async-done | bytes 204816 | tf_op jit(solution)/shard_map/reduce_scatter | solution.py:288
  (244 shorter events, 76.4 us)
Async XLA Ops:
  8.0 13.7 %copy-start.50 = (bf16[160,320]{1,0:T(8,128)(2,1)S(1)}, bf16[160,320]{1,0:T(8,128)(2,1)}, u32[]{:S(2)}) copy-start(bf16[160,320]{1,0:T(8,128)(2,1)} %param.28) | copy-start | bytes 307204
  8.0 25.3 %copy-start.51 = (bf16[160,320]{1,0:T(8,128)(2,1)S(1)}, bf16[160,320]{1,0:T(8,128)(2,1)}, u32[]{:S(2)}) copy-start(bf16[160,320]{1,0:T(8,128)(2,1)} %param.27) | copy-start | bytes 307204
  8.0 59.9 %all-gather.8.cloned.1.call-start = ((), (), s32[]{:S(2)}) async-start(), calls=%async_computation.11 | async-start | bytes 3276800 | tf_op jit(solution)/shard_map/all_gather | solution.py:188
  8.8 189.7 %reduce-scatter.18.cloned.1.call-start = ((), (), s32[]{:S(2)}) async-start(), calls=%async_computation.12 | async-start | bytes 6553600 | tf_op jit(solution)/shard_map/reduce_scatter | solution.py:206
  9.0 35.8 %copy-start.52 = (bf16[160,320]{1,0:T(8,128)(2,1)S(1)}, bf16[160,320]{1,0:T(8,128)(2,1)}, u32[]{:S(2)}) copy-start(bf16[160,320]{1,0:T(8,128)(2,1)} %param.30) | copy-start | bytes 307204
  21.8 70.9 %copy-start.24 = (bf16[1280,320]{1,0:T(8,128)(2,1)}, bf16[1280,320]{1,0:T(8,128)(2,1)S(1)}, u32[]{:S(2)}) copy-start(bf16[1280,320]{1,0:T(8,128)(2,1)S(1)} %all_gather.41) | copy-start | bytes 2457604
  83.3 4.2 copy-start.10
  87.5 6.3 copy-start.33
  87.5 6.3 copy-start.35
  89.5 6.5 copy-start
  93.8 5.1 copy-start.42
  94.9 4.1 copy-start.1
  105.8 94.3 %copy-start.49 = (f32[1280]{0:T(1024)S(1)}, f32[1280]{0:T(1024)}, u32[]{:S(2)}) copy-start(f32[1280]{0:T(1024)} %param.37) | copy-start | bytes 15364
  105.8 98.7 %all-gather.14.cloned.1.call-start = ((), (), s32[]{:S(2)}) async-start(), calls=%async_computation.15 | async-start | bytes 3686400 | tf_op jit(solution)/shard_map/all_gather | solution.py:166
  106.4 151.4 %all-gather.10.cloned.1.call-start = ((), (), s32[]{:S(2)}) async-start(), calls=%async_computation.13 | async-start | bytes 3276800 | tf_op jit(solution)/shard_map/all_gather | solution.py:214
  202.8 88.0 %all-gather.12.cloned.1.call-start = ((), (), s32[]{:S(2)}) async-start(), calls=%async_computation.14 | async-start | bytes 3686400 | tf_op jit(solution)/shard_map/all_gather | solution.py:165
  203.4 122.0 %all-gather.16.cloned.1.call-start = ((), (), s32[]{:S(2)}) async-start(), calls=%async_computation.16 | async-start | bytes 3686400 | tf_op jit(solution)/shard_map/all_gather | solution.py:167
  204.1 86.7 %copy-start.57 = (f32[1280]{0:T(1024)S(1)}, f32[1280]{0:T(1024)}, u32[]{:S(2)}) copy-start(f32[1280]{0:T(1024)} %param.35) | copy-start | bytes 15364
  204.1 86.7 %copy-start.58 = (f32[1280]{0:T(1024)S(1)}, f32[1280]{0:T(1024)}, u32[]{:S(2)}) copy-start(f32[1280]{0:T(1024)} %param.36) | copy-start | bytes 15364
  204.1 223.9 %reduce-scatter.20.cloned.1.call-start = ((), (), s32[]{:S(2)}) async-start(), calls=%async_computation.17 | async-start | bytes 6553600 | tf_op jit(solution)/shard_map/reduce_scatter | solution.py:221
  334.1 95.6 %copy-start.48 = (f32[1280]{0:T(1024)S(1)}, f32[1280]{0:T(1024)}, u32[]{:S(2)}) copy-start(f32[1280]{0:T(1024)} %param.38) | copy-start | bytes 15364
  334.1 155.9 %all-gather.18.cloned.1.call-start = ((), (), s32[]{:S(2)}) async-start(), calls=%async_computation.18 | async-start | bytes 3276800 | tf_op jit(solution)/shard_map/all_gather | solution.py:231
  434.9 168.5 %reduce-scatter.22.cloned.1.call-start = ((), (), s32[]{:S(2)}) async-start(), calls=%async_computation.19 | async-start | bytes 6553600 | tf_op jit(solution)/shard_map/reduce_scatter | solution.py:243
  490.0 11.1 copy-start.55
  501.1 3.6 copy-start.60
  501.1 3.8 copy-start.59
  501.1 4.4 copy-start.54
  510.9 154.7 %all-gather.20.cloned.1.call-start = ((), (), s32[]{:S(2)}) async-start(), calls=%async_computation.20 | async-start | bytes 3276800 | tf_op jit(solution)/shard_map/all_gather | solution.py:255
  609.4 56.2 %copy-start.30 = (bf16[1280,320]{1,0:T(8,128)(2,1)S(1)}, bf16[1280,320]{1,0:T(8,128)(2,1)}, u32[]{:S(2)}) copy-start(bf16[1280,320]{1,0:T(8,128)(2,1)} %all_gather.44) | copy-start | bytes 2457604
  610.5 58.6 %copy-start.43 = (bf16[512,320]{0,1:T(8,128)(2,1)S(1)}, bf16[512,320]{0,1:T(8,128)(2,1)}, u32[]{:S(2)}) copy-start(bf16[512,320]{0,1:T(8,128)(2,1)} %copy-done.42) | copy-start | bytes 983044
  610.5 234.9 %reduce-scatter.24.cloned.1.call-start = ((), (), s32[]{:S(2)}) async-start(), calls=%async_computation.21 | async-start | bytes 3276800 | tf_op jit(solution)/shard_map/reduce_scatter | solution.py:281
  669.1 4.5 copy-start.40
  669.1 10.7 slice-start
  669.1 10.7 slice-start.1
  673.7 4.2 copy-start.36
  673.7 6.1 slice-start.2
  683.9 3.3 copy-start.15
  695.2 7.7 slice-start.3
  705.3 6.0 copy-start.28
  714.6 3.9 copy-start.25
  721.8 125.9 %reduce-scatter.28.cloned.1.call-start = ((), (), s32[]{:S(2)}) async-start(), calls=%async_computation.23 | async-start | bytes 7372800 | tf_op jit(solution)/shard_map/reduce_scatter | solution.py:247
  730.8 176.0 %reduce-scatter.30.cloned.1.call-start = ((), (), s32[]{:S(2)}) async-start(), calls=%async_computation.24 | async-start | bytes 7372800 | tf_op jit(solution)/shard_map/reduce_scatter | solution.py:248
  740.7 233.0 %reduce-scatter.32.cloned.1.call-start = ((), (), s32[]{:S(2)}) async-start(), calls=%async_computation.25 | async-start | bytes 7372800 | tf_op jit(solution)/shard_map/reduce_scatter | solution.py:249
  749.6 268.0 %reduce-scatter.34.cloned.1.call-start = ((), (), s32[]{:S(2)}) async-start(), calls=%async_computation.26 | async-start | bytes 2211840
  757.5 304.2 %reduce-scatter.36.cloned.1.call-start = ((), (), s32[]{:S(2)}) async-start(), calls=%async_computation.27 | async-start | bytes 2211840
  765.3 340.3 %reduce-scatter.38.cloned.1.call-start = ((), (), s32[]{:S(2)}) async-start(), calls=%async_computation.28 | async-start | bytes 2211840
  773.1 376.6 %reduce-scatter.26.cloned.1.call-start = ((), (), s32[]{:S(2)}) async-start(), calls=%async_computation.22 | async-start | bytes 2211840 | tf_op jit(solution)/shard_map/reduce_scatter | solution.py:288
  820.0 25.4 %copy-start.13 = (f32[256,1280]{1,0:T(8,128)S(1)}, f32[256,1280]{1,0:T(8,128)}, u32[]{:S(2)}) copy-start(f32[256,1280]{1,0:T(8,128)} %copy-done.12) | copy-start | bytes 3932164
  (36 other events, 56.8 us)
Sparse Core Ops, SparseCore 0:
  10.4 57.4 all-gather.7
  105.9 92.5 reduce-scatter.17
  334.2 93.7 reduce-scatter.19
  511.0 92.3 reduce-scatter.21
Sparse Core Ops, SparseCore 1:
  108.2 31.4 all-gather.13
  202.9 54.9 all-gather.9
  259.6 31.2 all-gather.11
  292.7 32.6 all-gather.15
  435.0 54.9 all-gather.17
  610.6 54.9 all-gather.19
  721.9 50.8 reduce-scatter.23
  776.6 63.3 reduce-scatter.27
  843.9 62.9 reduce-scatter.29
  910.8 62.8 reduce-scatter.31
  977.6 40.0 reduce-scatter.33
  1021.6 40.0 reduce-scatter.35
  1065.6 40.0 reduce-scatter.37
  1109.6 40.0 reduce-scatter.25
where the time goes:
time: 1160 us
  waiting for transfers between devices  805 us (69%)
  matrix products  153 us (13%)
  blocking collectives  112 us (10%)
  other arithmetic  43.9 us (4%)
  local copies, waits for them, and re-layouts  24.4 us (2%)
  between operations  16.9 us (1%)
    unnamed x21, waiting for transfers between devices  135 us
    reduce_scatter x1, waiting for transfers between devices, on_device(): lax.psum_scatter(contract_cols(hidden_low, down_w), 'tensor', scatter_dim...  93.9 us
    reduce_scatter x1, waiting for transfers between devices, on_device(): lax.psum_scatter(g_mid_part, 'tensor', scatter_dimension=0, tiled=True)  92.5 us
    reduce_scatter x1, waiting for transfers between devices, on_device(): lax.psum_scatter(contract_cols(attended_low, out_w), 'tensor', scatter_di...  92.1 us
    reduce_scatter x1, waiting for transfers between devices, on_device(): lax.psum_scatter(down_grad, 'dp', scatter_dimension=0, tiled=True)  66.9 us
    reduce_scatter x1, waiting for transfers between devices, on_device(): lax.psum_scatter(gate_grad, 'dp', scatter_dimension=0, tiled=True)  59.1 us
    all_gather x1, waiting for transfers between devices, on_device(): g_attn_whole = lax.all_gather(g_attn_low, 'tensor', axis=0, tiled=True)  54.8 us
    all_gather x1, waiting for transfers between devices, on_device(): g_mlp_whole = lax.all_gather(g_mlp_low, 'tensor', axis=0, tiled=True)  54.5 us
  transfers between devices with their start and end apart: 18, of which 15 were waited for; matrix products, arithmetic and copies ran while one was open for 7% of the time, Pallas kernels for 0%

commit v1 on v0

--- a/solution.py
+++ b/solution.py
@@ -2,10 +2,37 @@
 import jax.numpy as jnp
 from jax import lax
 from jax.sharding import PartitionSpec as P
+from jax.lax import axis_index, ppermute, psum
 
 HEAD_DIM = 64
 HIGH = lax.Precision.HIGHEST
 EPS = 1e-06
+
+
+def launch_lane(values, dim_at):
+    values = jnp.moveaxis(values, 0, dim_at)
+    taken_in = values.shape
+    return values.reshape(
+        *taken_in[:dim_at], taken_in[dim_at] * taken_in[dim_at + 1], *taken_in[dim_at + 2 :]
+    )
+
+
+def _mark_blocks(z, which_axis):
+    field_out, oldest = (psum(1, axis_name=which_axis), axis_index(which_axis))
+    next_value, n_now = (z[None], 1)
+    while n_now < field_out:
+        block_out = ppermute(
+            next_value, axis_name=which_axis, perm=[(dd, dd ^ n_now) for dd in range(field_out)]
+        )
+        piece_now = oldest & n_now == 0
+        next_value = jnp.concatenate(
+            [
+                jnp.where(piece_now, next_value, block_out),
+                jnp.where(piece_now, block_out, next_value),
+            ]
+        )
+        n_now *= 2
+    return next_value
 
 
 def unit_rows(value):
@@ -252,7 +279,11 @@
     g_alpha_attn = jnp.sum((attn_unit - residual) * g_first, axis=0)
     g_attn_low = unit_back(alpha_attn * g_first, attn_unit, attn_norm).astype(jnp.bfloat16)
     query_w, key_w, value_w, out_w = gather_attention(w_query, w_key, w_value, w_out)
-    g_attn_whole = lax.all_gather(g_attn_low, "tensor", axis=0, tiled=True)
+
+    def switch_block(inputs, my_tile, which_dim):
+        return launch_lane(_mark_blocks(inputs, my_tile), which_dim)
+
+    g_attn_whole = switch_block(g_attn_low, "tensor", 0)
     out_grad = contract_rows(g_attn_whole, attended_low)
     g_attended_low = jnp.dot(g_attn_whole, out_w, preferred_element_type=jnp.float32).astype(
         jnp.bfloat16

time: 1160 us -> 1190 us (1.026)
  waiting for transfers between devices: 805 us -> 821 us
    ppermute x0 -> x2, waiting for transfers between devices: none -> 71 us  [_mark_blocks(): ppermute(next_value, axis_name=which_axis, perm=[(dd, dd ^ n_now) for dd...]
    all_gather x1 -> x0, waiting for transfers between devices: 54.8 us -> none  [on_device(): g_attn_whole = lax.all_gather(g_attn_low, 'tensor', axis=0, tiled=True)]
    unnamed x135 -> x173, local copies, waits for them, and re-layouts: 22.6 us -> 26.4 us
    unnamed x21 -> x20, waiting for transfers between devices: 135 us -> 135 us
  transfers between devices with their start and end apart: 18 -> 19, of which waited for: 15 -> 16; matrix products, arithmetic and copies ran while one was open for 7% -> 7% of each run, Pallas kernels for 0% -> 0%
where the time goes in v1:
time: 1190 us
  waiting for transfers between devices  821 us (69%)
  matrix products  155 us (13%)
  blocking collectives  111 us (9%)
  other arithmetic  47.3 us (4%)
  local copies, waits for them, and re-layouts  28.2 us (2%)
  between operations  16.9 us (1%)
    unnamed x20, waiting for transfers between devices  135 us
    reduce_scatter x1, waiting for transfers between devices, on_device(): lax.psum_scatter(contract_cols(hidden_low, down_w), 'tensor', scatter_dim...  93.9 us
    reduce_scatter x1, waiting for transfers between devices, on_device(): lax.psum_scatter(g_mid_part, 'tensor', scatter_dimension=0, tiled=True)  92.5 us
    reduce_scatter x1, waiting for transfers between devices, on_device(): lax.psum_scatter(contract_cols(attended_low, out_w), 'tensor', scatter_di...  92.1 us
    ppermute x2, waiting for transfers between devices, _mark_blocks(): ppermute(next_value, axis_name=which_axis, perm=[(dd, dd ^ n_now) for dd...  71 us
    reduce_scatter x1, waiting for transfers between devices, on_device(): lax.psum_scatter(down_grad, 'dp', scatter_dimension=0, tiled=True)  66.8 us
    reduce_scatter x1, waiting for transfers between devices, on_device(): lax.psum_scatter(gate_grad, 'dp', scatter_dimension=0, tiled=True)  58.9 us
    all_gather x1, waiting for transfers between devices, on_device(): g_mlp_whole = lax.all_gather(g_mlp_low, 'tensor', axis=0, tiled=True)  54.6 us
  transfers between devices with their start and end apart: 19, of which 16 were waited for; matrix products, arithmetic and copies ran while one was open for 7% of the time, Pallas kernels for 0%

profile of v1, /device:TPU:0, one launch (start us, length us, event | category | flops | bytes accessed | tf_op | source)
XLA Modules:
  0.0 1185.6 jit_solution(11223314024236230291)
XLA Ops:
  9.0 12.7 %all_gather.38 = bf16[1280,320]{1,0:T(8,128)(2,1)S(1)} all-gather(bf16[160,320]{1,0:T(8,128)(2,1)} %param.29), channel_id=1, replica_groups=mesh['dp'=8,'tensor'=4] {'dp'}, dimensions={0}, use_global_device_ids=true | all-gather | bytes 921600 | tf_op jit(solution)/shard_map/all_gather | solution.py:185
  21.7 10.9 all_gather.40
  32.5 11.4 all_gather.39
  44.0 11.5 all_gather.41
  55.8 12.1 %all-gather.7.cloned.1.call-done = bf16[1024,1280]{1,0:T(8,128)(2,1)} async-done(((bf16[256,1280]{1,0:T(8,128)(2,1)}), bf16[1024,1280]{1,0:T(8,128)(2,1)}) %all-gather.7.cloned.1.call-update) | async-done | bytes 2621456 | tf_op jit(solution)/shard_map/all_gather | solution.py:215
  74.1 6.9 fusion.20
  85.0 2.9 multiply_convert_fusion.7
  90.0 3.1 exponential_reduce_fusion
  96.5 2.9 convolution_convert_fusion.2
  102.3 3.9 fusion.129
  106.8 92.1 %reduce-scatter.18.cloned.1.call-done = f32[256,1280]{1,0:T(8,128)} async-done(((f32[1024,1280]{1,0:T(8,128)}), f32[256,1280]{1,0:T(8,128)}) %reduce-scatter.18.cloned.1.call-update) | async-done | bytes 1310736 | tf_op jit(solution)/shard_map/reduce_scatter | solution.py:233
  204.8 53.4 %all-gather.9.cloned.1.call-done = bf16[1024,1280]{1,0:T(8,128)(2,1)} async-done(((bf16[256,1280]{1,0:T(8,128)(2,1)}), bf16[1024,1280]{1,0:T(8,128)(2,1)}) %all-gather.9.cloned.1.call-update) | async-done | bytes 2621456 | tf_op jit(solution)/shard_map/all_gather | solution.py:241
  258.2 8.6 fusion.130
  266.8 24.4 %all-gather.11.cloned.1.call-done = bf16[1280,1280]{1,0:T(8,128)(2,1)} async-done(((bf16[160,1280]{1,0:T(8,128)(2,1)}), bf16[1280,1280]{1,0:T(8,128)(2,1)}) %all-gather.11.cloned.1.call-update) | async-done | bytes 3276816 | tf_op jit(solution)/shard_map/all_gather | solution.py:192
  291.2 11.3 multiply_convert_fusion.4
  302.5 23.2 %all-gather.15.cloned.1.call-done = bf16[1280,1280]{1,0:T(8,128)(2,1)} async-done(((bf16[160,1280]{1,0:T(8,128)(2,1)}), bf16[1280,1280]{1,0:T(8,128)(2,1)}) %all-gather.15.cloned.1.call-update) | async-done | bytes 3276816 | tf_op jit(solution)/shard_map/all_gather | solution.py:194
  325.8 8.6 fusion.131
  334.4 93.9 %reduce-scatter.20.cloned.1.call-done = f32[256,1280]{1,0:T(8,128)} async-done(((f32[1024,1280]{1,0:T(8,128)}), f32[256,1280]{1,0:T(8,128)}) %reduce-scatter.20.cloned.1.call-update) | async-done | bytes 1310736 | tf_op jit(solution)/shard_map/reduce_scatter | solution.py:248
  436.3 54.6 %all-gather.17.cloned.1.call-done = bf16[1024,1280]{1,0:T(8,128)(2,1)} async-done(((bf16[256,1280]{1,0:T(8,128)(2,1)}), bf16[1024,1280]{1,0:T(8,128)(2,1)}) %all-gather.17.cloned.1.call-update) | async-done | bytes 2621456 | tf_op jit(solution)/shard_map/all_gather | solution.py:258
  490.9 11.7 multiply_reduce_fusion.1
  502.6 3.6 fusion.132
  506.9 5.4 convolution_add_fusion
  512.4 92.5 %reduce-scatter.22.cloned.1.call-done = f32[256,1280]{1,0:T(8,128)} async-done(((f32[1024,1280]{1,0:T(8,128)}), f32[256,1280]{1,0:T(8,128)}) %reduce-scatter.22.cloned.1.call-update) | async-done | bytes 1310736 | tf_op jit(solution)/shard_map/reduce_scatter | solution.py:270
  611.5 14.9 %collective-permute-done = bf16[1,256,1280]{2,1,0:T(8,128)(2,1)S(1)} collective-permute-done((bf16[1,256,1280]{2,1,0:T(8,128)(2,1)S(1)}, bf16[1,256,1280]{2,1,0:T(8,128)(2,1)S(1)}, u32[]{:S(2)}, u32[]{:S(2)}) %collective-permute-start) | collective-permute-done | bytes 655392 | tf_op jit(solution)/shard_map/ppermute | solution.py:24
  627.8 3.0 collective-permute-start.1
  630.8 56.1 %collective-permute-done.1 = bf16[2,256,1280]{2,1,0:T(8,128)(2,1)} collective-permute-done((bf16[2,256,1280]{2,1,0:T(8,128)(2,1)S(1)}, bf16[2,256,1280]{2,1,0:T(8,128)(2,1)}, u32[]{:S(2)}, u32[]{:S(2)}) %collective-permute-start.1) | collective-permute-done | bytes 1310752 | tf_op jit(solution)/shard_map/ppermute | solution.py:24
  694.1 2.8 multiply_convert_fusion.1
  699.7 6.4 multiply_reduce_fusion
  706.1 6.1 multiply_convert_fusion
  721.8 7.4 fusion.35
  732.8 5.6 fusion.24
  741.7 3.0 fusion.12
  745.5 3.3 add_convert_fusion
  749.4 8.8 fusion.135
  758.9 9.7 fusion.66
  768.6 8.9 fusion.136
  778.6 4.0 convolution_bitcast_fusion.2
  786.4 3.9 convolution_bitcast_fusion.1
  794.3 3.9 convolution_bitcast_fusion
  802.1 4.6 fusion.68
  807.4 39.4 %all-reduce.2 = (f32[1280]{0:T(1024)}, f32[1280]{0:T(1024)}) all-reduce(f32[1280]{0:T(1024)S(1)} %copy-done.62, f32[1280]{0:T(1024)S(1)} %copy-done.61), channel_id=1, replica_groups=mesh['dp'=8,'tensor'=4] {'dp','tensor'}, use_global_device_ids=true, to_apply=%region_33.34 | all-reduce | flops 2560 | bytes 20480 | tf_op jit(solution)/shard_map/psum | solution.py:324
  849.2 25.0 %all-reduce.3 = (f32[320]{0:T(512)}, f32[1280]{0:T(1024)}, f32[1280]{0:T(1024)}) all-reduce(f32[320]{0:T(512)S(1)} %add.253, f32[1280]{0:T(1024)S(1)} %copy-done.68, f32[1280]{0:T(1024)S(1)} %copy-done.67), channel_id=1, replica_groups=mesh['dp'=8,'tensor'=4] {'dp'}, use_global_device_ids=true, to_apply=%region_27.28 | all-reduce | flops 2880 | bytes 23040 | tf_op jit(solution)/shard_map/psum | solution.py:321
  876.5 58.9 %reduce-scatter.30.cloned.1.call-done = f32[160,1280]{1,0:T(8,128)} async-done(((f32[1280,1280]{1,0:T(8,128)}), f32[160,1280]{1,0:T(8,128)}) %reduce-scatter.30.cloned.1.call-update) | async-done | bytes 819216 | tf_op jit(solution)/shard_map/reduce_scatter | solution.py:275
  935.4 66.8 %reduce-scatter.32.cloned.1.call-done = f32[160,1280]{1,0:T(8,128)} async-done(((f32[1280,1280]{1,0:T(8,128)}), f32[160,1280]{1,0:T(8,128)}) %reduce-scatter.32.cloned.1.call-update) | async-done | bytes 819216 | tf_op jit(solution)/shard_map/reduce_scatter | solution.py:276
  1002.1 44.1 %reduce-scatter.34.cloned.1.call-done = f32[160,320]{1,0:T(8,128)} async-done(((f32[1280,320]{1,0:T(8,128)}), f32[160,320]{1,0:T(8,128)}) %reduce-scatter.34.cloned.1.call-update) | async-done | bytes 204816
  1046.2 43.9 %reduce-scatter.36.cloned.1.call-done = f32[160,320]{1,0:T(8,128)} async-done(((f32[1280,320]{1,0:T(8,128)}), f32[160,320]{1,0:T(8,128)}) %reduce-scatter.36.cloned.1.call-update) | async-done | bytes 204816
  1090.1 44.1 %reduce-scatter.38.cloned.1.call-done = f32[160,320]{1,0:T(8,128)} async-done(((f32[1280,320]{1,0:T(8,128)}), f32[160,320]{1,0:T(8,128)}) %reduce-scatter.38.cloned.1.call-update) | async-done | bytes 204816
  1134.2 43.9 %reduce-scatter.26.cloned.1.call-done = f32[160,320]{1,0:T(8,128)} async-done(((f32[1280,320]{1,0:T(8,128)}), f32[160,320]{1,0:T(8,128)}) %reduce-scatter.26.cloned.1.call-update) | async-done | bytes 204816 | tf_op jit(solution)/shard_map/reduce_scatter | solution.py:319
  (287 shorter events, 88.9 us)
Async XLA Ops:
  8.0 13.7 %copy-start.57 = (bf16[160,320]{1,0:T(8,128)(2,1)S(1)}, bf16[160,320]{1,0:T(8,128)(2,1)}, u32[]{:S(2)}) copy-start(bf16[160,320]{1,0:T(8,128)(2,1)} %param.28) | copy-start | bytes 307204
  8.0 59.9 %all-gather.7.cloned.1.call-start = ((), (), s32[]{:S(2)}) async-start(), calls=%async_computation.11 | async-start | bytes 3276800 | tf_op jit(solution)/shard_map/all_gather | solution.py:215
  8.8 23.8 %copy-start.58 = (bf16[160,320]{1,0:T(8,128)(2,1)S(1)}, bf16[160,320]{1,0:T(8,128)(2,1)}, u32[]{:S(2)}) copy-start(bf16[160,320]{1,0:T(8,128)(2,1)} %param.27) | copy-start | bytes 307204
  8.8 190.1 %reduce-scatter.18.cloned.1.call-start = ((), (), s32[]{:S(2)}) async-start(), calls=%async_computation.12 | async-start | bytes 6553600 | tf_op jit(solution)/shard_map/reduce_scatter | solution.py:233
  8.8 65.3 %copy-start.69 = (pred[320]{0:T(512)(128)(4,1)}, pred[320]{0:T(512)(128)(4,1)S(1)}, u32[]{:S(2)}) copy-start(pred[320]{0:T(512)(128)(4,1)S(1)} %fusion.108) | copy-start | bytes 964
  8.8 76.1 %copy-start.63 = (pred[320]{0:T(512)(128)(4,1)}, pred[320]{0:T(512)(128)(4,1)S(1)}, u32[]{:S(2)}) copy-start(pred[320]{0:T(512)(128)(4,1)S(1)} %fusion.110) | copy-start | bytes 964
  8.9 65.2 %copy-start.65 = (f32[320]{0:T(512)}, f32[320]{0:T(512)S(1)}, u32[]{:S(2)}) copy-start(f32[320]{0:T(512)S(1)} %fusion.104) | copy-start | bytes 3844
  9.0 682.6 %copy-start.16 = (pred[512,512]{0,1:T(8,128)(4,1)}, pred[512,512]{0,1:T(8,128)(4,1)S(1)}, u32[]{:S(2)}) copy-start(pred[512,512]{0,1:T(8,128)(4,1)S(1)} %iota_compare_fusion.1) | copy-start | bytes 786436
  21.7 71.4 %copy-start.25 = (bf16[1280,320]{1,0:T(8,128)(2,1)}, bf16[1280,320]{1,0:T(8,128)(2,1)S(1)}, u32[]{:S(2)}) copy-start(bf16[1280,320]{1,0:T(8,128)(2,1)S(1)} %all_gather.38) | copy-start | bytes 2457604
  21.7 22.3 %copy-start.59 = (bf16[160,320]{1,0:T(8,128)(2,1)S(1)}, bf16[160,320]{1,0:T(8,128)(2,1)}, u32[]{:S(2)}) copy-start(bf16[160,320]{1,0:T(8,128)(2,1)} %param.30) | copy-start | bytes 307204
  32.5 35.4 %copy-start.27 = (bf16[1280,320]{1,0:T(8,128)(2,1)}, bf16[1280,320]{1,0:T(8,128)(2,1)S(1)}, u32[]{:S(2)}) copy-start(bf16[1280,320]{1,0:T(8,128)(2,1)S(1)} %all_gather.40) | copy-start | bytes 2457604
  83.4 4.5 copy-start.10
  88.0 6.3 copy-start.35
  88.0 6.3 copy-start.37
  90.0 6.5 copy-start
  94.3 5.2 copy-start.45
  95.3 4.1 copy-start.1
  106.2 94.3 %copy-start.56 = (f32[1280]{0:T(1024)S(1)}, f32[1280]{0:T(1024)}, u32[]{:S(2)}) copy-start(f32[1280]{0:T(1024)} %param.37) | copy-start | bytes 15364
  106.2 98.6 %all-gather.13.cloned.1.call-start = ((), (), s32[]{:S(2)}) async-start(), calls=%async_computation.15 | async-start | bytes 3686400 | tf_op jit(solution)/shard_map/all_gather | solution.py:193
  106.8 151.4 %all-gather.9.cloned.1.call-start = ((), (), s32[]{:S(2)}) async-start(), calls=%async_computation.13 | async-start | bytes 3276800 | tf_op jit(solution)/shard_map/all_gather | solution.py:241
  203.2 88.0 %all-gather.11.cloned.1.call-start = ((), (), s32[]{:S(2)}) async-start(), calls=%async_computation.14 | async-start | bytes 3686400 | tf_op jit(solution)/shard_map/all_gather | solution.py:192
  203.8 122.0 %all-gather.15.cloned.1.call-start = ((), (), s32[]{:S(2)}) async-start(), calls=%async_computation.16 | async-start | bytes 3686400 | tf_op jit(solution)/shard_map/all_gather | solution.py:194
  204.5 86.7 %copy-start.74 = (f32[1280]{0:T(1024)S(1)}, f32[1280]{0:T(1024)}, u32[]{:S(2)}) copy-start(f32[1280]{0:T(1024)} %param.35) | copy-start | bytes 15364
  204.5 86.7 %copy-start.75 = (f32[1280]{0:T(1024)S(1)}, f32[1280]{0:T(1024)}, u32[]{:S(2)}) copy-start(f32[1280]{0:T(1024)} %param.36) | copy-start | bytes 15364
  204.5 223.8 %reduce-scatter.20.cloned.1.call-start = ((), (), s32[]{:S(2)}) async-start(), calls=%async_computation.17 | async-start | bytes 6553600 | tf_op jit(solution)/shard_map/reduce_scatter | solution.py:248
  334.3 95.6 %copy-start.55 = (f32[1280]{0:T(1024)S(1)}, f32[1280]{0:T(1024)}, u32[]{:S(2)}) copy-start(f32[1280]{0:T(1024)} %param.38) | copy-start | bytes 15364
  334.4 156.5 %all-gather.17.cloned.1.call-start = ((), (), s32[]{:S(2)}) async-start(), calls=%async_computation.18 | async-start | bytes 3276800 | tf_op jit(solution)/shard_map/all_gather | solution.py:258
  435.8 169.1 %reduce-scatter.22.cloned.1.call-start = ((), (), s32[]{:S(2)}) async-start(), calls=%async_computation.19 | async-start | bytes 6553600 | tf_op jit(solution)/shard_map/reduce_scatter | solution.py:270
  490.9 11.7 copy-start.72
  502.5 4.4 copy-start.71
  512.3 361.9 %reduce-scatter.24.cloned.1.call-start = ((), (), s32[]{:S(2)}) async-start(), calls=%async_computation.20 | async-start | bytes 3276800 | tf_op jit(solution)/shard_map/reduce_scatter | solution.py:312
  610.0 16.4 %collective-permute-start = (bf16[1,256,1280]{2,1,0:T(8,128)(2,1)S(1)}, bf16[1,256,1280]{2,1,0:T(8,128)(2,1)S(1)}, u32[]{:S(2)}, u32[]{:S(2)}) collective-permute-start(bf16[1,256,1280]{2,1,0:T(8,128)(2,1)S(1)} %fusion.67), channel_id=1, source_target_pairs={{0,1},{1,0},{2,3},{3,2},{4,5},{5,4},{6,7},{7,6},{8,9},{9,8},{10,11... | collective-permute-start | bytes 1966088 | tf_op jit(solution)/shard_map/ppermute | solution.py:24
  627.8 59.1 %collective-permute-start.1 = (bf16[2,256,1280]{2,1,0:T(8,128)(2,1)S(1)}, bf16[2,256,1280]{2,1,0:T(8,128)(2,1)}, u32[]{:S(2)}, u32[]{:S(2)}) collective-permute-start(bf16[2,256,1280]{2,1,0:T(8,128)(2,1)S(1)} %pad_maximum_fusion.1), channel_id=1, source_target_pairs={{0,2},{1,3},{2,0},{3,1},{4,6},{5,7},{6,4},{7,5},{8,10},{9,11},{10,... | collective-permute-start | bytes 3932168 | tf_op jit(solution)/shard_map/ppermute | solution.py:24
  686.8 4.8 slice-start.3
  691.9 7.5 slice-start
  691.9 7.6 slice-start.1
  694.1 5.4 slice-start.2
  706.1 6.1 copy-start.15
  732.8 5.6 copy-start.30
  741.7 3.9 copy-start.26
  748.9 127.6 %reduce-scatter.28.cloned.1.call-start = ((), (), s32[]{:S(2)}) async-start(), calls=%async_computation.22 | async-start | bytes 7372800 | tf_op jit(solution)/shard_map/reduce_scatter | solution.py:274
  758.2 177.1 %reduce-scatter.30.cloned.1.call-start = ((), (), s32[]{:S(2)}) async-start(), calls=%async_computation.23 | async-start | bytes 7372800 | tf_op jit(solution)/shard_map/reduce_scatter | solution.py:275
  768.6 233.5 %reduce-scatter.32.cloned.1.call-start = ((), (), s32[]{:S(2)}) async-start(), calls=%async_computation.24 | async-start | bytes 7372800 | tf_op jit(solution)/shard_map/reduce_scatter | solution.py:276
  777.5 268.7 %reduce-scatter.34.cloned.1.call-start = ((), (), s32[]{:S(2)}) async-start(), calls=%async_computation.25 | async-start | bytes 2211840
  785.4 304.7 %reduce-scatter.36.cloned.1.call-start = ((), (), s32[]{:S(2)}) async-start(), calls=%async_computation.26 | async-start | bytes 2211840
  793.2 341.0 %reduce-scatter.38.cloned.1.call-start = ((), (), s32[]{:S(2)}) async-start(), calls=%async_computation.27 | async-start | bytes 2211840
  801.0 377.1 %reduce-scatter.26.cloned.1.call-start = ((), (), s32[]{:S(2)}) async-start(), calls=%async_computation.21 | async-start | bytes 2211840 | tf_op jit(solution)/shard_map/reduce_scatter | solution.py:319
  848.5 25.7 %copy-start.13 = (f32[256,1280]{1,0:T(8,128)S(1)}, f32[256,1280]{1,0:T(8,128)}, u32[]{:S(2)}) copy-start(f32[256,1280]{1,0:T(8,128)} %copy-done.12) | copy-start | bytes 3932164
  (56 other events, 89.8 us)
Sparse Core Ops, SparseCore 0:
  10.4 57.4 all-gather.6
  106.3 92.5 reduce-scatter.17
  334.5 93.7 reduce-scatter.19
  512.5 92.3 reduce-scatter.21
Sparse Core Ops, SparseCore 1:
  108.6 31.4 all-gather.12
  203.3 54.9 all-gather.8
  260.0 31.2 all-gather.10
  293.1 32.6 all-gather.14
  435.9 54.9 all-gather.16
  749.0 52.3 reduce-scatter.23
  805.2 63.3 reduce-scatter.27
  872.4 62.8 reduce-scatter.29
  939.3 62.8 reduce-scatter.31
  1006.1 40.0 reduce-scatter.33
  1050.1 40.0 reduce-scatter.35
  1094.1 40.0 reduce-scatter.37
  1138.0 40.0 reduce-scatter.25
